TPU v7x, 32 devices: a 4x4x1 block of a 4x4x8 slice. The times are simulated.
32 devices in a mesh: ens: 1 (over z), sp: 32 (over y, x, core).
Axes of the slice: x: 4, y: 4, z: 1, core: 2. Of those that a mesh axis runs over, the one named last changes fastest.
The devices are a block of a 4x4x8 slice.
Arguments:
- x_seq: bfloat16 [16384, 512], P(('ens', 'sp'))
- w_past: bfloat16 [3, 10, 512, 1024], replicated
- w_now: bfloat16 [3, 10, 512, 1024], replicated
- b_conv: float32 [3, 10, 1024], replicated
- w_res: bfloat16 [3, 10, 512, 512], replicated
- w_skip: bfloat16 [3, 10, 512, 256], replicated
- w_out1: bfloat16 [256, 256], replicated
- b_out1: float32 [256], replicated
- w_out2: bfloat16 [256, 256], replicated
- b_out2: float32 [256], replicated
Outputs:
- output 1: float32 [16384, 256], P(('ens', 'sp'))
- output 2: bfloat16 [16384, 512], P(('ens', 'sp'))
All inputs are finite; a program needn't handle non-finite values.
Results may differ from a plain program's by a relative error of at most 0.02.
Values are sent between devices in bfloat16 or wider.
A program may use at most 768 MiB of HBM per device.

v0:
```python
import functools

import jax
import jax.numpy as jnp
from jax import lax
from jax.experimental import pallas as pl
from jax.experimental.pallas import tpu as pltpu
from jax.sharding import PartitionSpec as P

TILE = 16
ROWS = 128
CHUNK = 256
MESH = pl.DeviceIdType.MESH


def halo_rows(k):
    return max(TILE, 2 ** k)


def wavenet_kernel(n_sp, stacks, cycle, x_ref, wp_ref, wn_ref, b_ref, wr_ref, ws_ref, w1_ref, c1_ref, w2_ref, c2_ref,
                   y_ref, hout_ref, hbuf, skip, wp, wn, wr, ws, stage, *scratch):
    halos, (x_sem, w_sem, send_sem, recv_sem, out_sem) = scratch[:cycle], scratch[cycle:]
    me = lax.axis_index("sp")
    ens = lax.axis_index("ens")
    right = lax.rem(me + 1, n_sp)
    left = lax.rem(me + n_sp - 1, n_sp)
    first = me == 0
    rows = hbuf.shape[0]
    gate = wr.shape[1]
    f32, bf16 = jnp.float32, jnp.bfloat16

    def weight_copies(stack, k):
        return [pltpu.make_async_copy(src.at[stack, k], dst.at[k], w_sem.at[k, i])
                for i, (src, dst) in enumerate(((wp_ref, wp), (wn_ref, wn), (wr_ref, wr), (ws_ref, ws)))]

    def pieces(k):
        lo = rows - halo_rows(k)
        out = []
        hi = rows
        while hi > lo:
            out.append((max(lo, hi - ROWS), hi))
            hi = max(lo, hi - ROWS)
        return out

    stage_off = []
    off = 0
    for k in range(cycle):
        stage_off.append(off)
        off += halo_rows(k)

    def send(stack, k, p):
        a, b = pieces(k)[p]
        lo = rows - halo_rows(k)
        return pltpu.make_async_remote_copy(
            src_ref=stage.at[pl.ds(stage_off[k] + a - lo, b - a)],
            dst_ref=halos[k].at[stack, pl.ds(a - lo, b - a)],
            send_sem=send_sem.at[k, p],
            recv_sem=recv_sem.at[stack, k, p],
            device_id=(ens, right),
            device_id_type=MESH,
        )

    x_copy = pltpu.make_async_copy(x_ref, hbuf, x_sem)
    x_copy.start()
    for k in range(cycle):
        for c in weight_copies(0, k):
            c.start()

    barrier = pltpu.get_barrier_semaphore()
    for other in (left, right):
        pl.semaphore_signal(barrier, inc=1, device_id=(ens, other), device_id_type=MESH)
    pl.semaphore_wait(barrier, 2)

    skip[...] = jnp.zeros_like(skip)
    x_copy.wait()

    blocks = [(r, r + ROWS) for r in range(rows - ROWS, -1, -ROWS)]
    units = [(k, r0, r1) for k in range(cycle) for (r0, r1) in blocks]

    def past_rows(stack, k, r0, r1):
        d = 2 ** k
        if d >= rows:
            return jnp.where(first, jnp.zeros((), bf16), halos[k][stack, r0:r1, :])
        if d >= TILE:
            a, b = r0 - d, r1 - d
            parts = []
            if a < 0:
                h = halo_rows(k)
                v = halos[k][stack, h + a:h + min(b, 0), :]
                parts.append(jnp.where(first, jnp.zeros((), bf16), v))
            if b > 0:
                parts.append(hbuf[max(a, 0):b, :])
            return parts[0] if len(parts) == 1 else jnp.concatenate(parts, axis=0)
        if r0 == 0:
            v = jnp.concatenate([jnp.where(first, jnp.zeros((), bf16), halos[k][stack]), hbuf[0:r1, :]], axis=0)
        else:
            v = hbuf[r0 - TILE:r1, :]
        v = v.astype(f32)[TILE - d:TILE - d + r1 - r0]
        return v.astype(bf16)

    def body(stack, carry):
        waited_w = set()
        waited_h = set()

        def conv(unit):
            k, r0, r1 = unit
            if k not in waited_w:
                waited_w.add(k)
                for c in weight_copies(stack, k):
                    c.wait()
            lo = rows - halo_rows(k)
            d = 2 ** k
            for p, (a, b) in enumerate(pieces(k)):
                need = (r0 - d < b - rows) and (r1 - d > a - rows)
                if need and (k, p) not in waited_h:
                    waited_h.add((k, p))
                    send(stack, k, p).wait_recv()
            past = past_rows(stack, k, r0, r1)
            now = hbuf[r0:r1, :]
            return past, now

        def conv_chunk(unit, lhs, c):
            k = unit[0]
            past, now = lhs
            out = []
            for base in (c * CHUNK, gate + c * CHUNK):
                z = jnp.dot(past, wp[k, :, base:base + CHUNK], preferred_element_type=f32)
                z = z + jnp.dot(now, wn[k, :, base:base + CHUNK], preferred_element_type=f32)
                out.append(z)
            return out

        def gated(unit, z, c):
            k = unit[0]
            bias = b_ref[stack, k]
            zt = z[0] + bias[None, c * CHUNK:(c + 1) * CHUNK]
            zs = z[1] + bias[None, gate + c * CHUNK:gate + (c + 1) * CHUNK]
            sig = 0.5 * jnp.tanh(0.5 * zs) + 0.5
            return (jnp.tanh(zt) * sig).astype(bf16)

        def finish(unit, g):
            k, r0, r1 = unit
            g = jnp.concatenate(g, axis=1)
            h = hbuf[r0:r1, :].astype(f32) + jnp.dot(g, wr[k], preferred_element_type=f32)
            h = h.astype(bf16)
            hbuf[r0:r1, :] = h
            skip[r0:r1, :] += jnp.dot(g, ws[k], preferred_element_type=f32)
            nk = k + 1
            nstack = stack
            if nk == cycle:
                nk = 0
            lo = rows - halo_rows(nk)
            todo = [(p, a, b) for p, (a, b) in enumerate(pieces(nk)) if a >= r0 and b <= r1]

            def go():
                for p, a, b in todo:
                    o = stage_off[nk] + a - lo
                    send_done(nk, p)
                    stage[o:o + b - a, :] = h[a - r0:b - r0]
                    send(stack + (1 if k + 1 == cycle else 0), nk, p).start()

            def send_done(nk, p):
                if nk == 0:
                    send(stack, nk, p).wait_send()

            if todo:
                if k + 1 == cycle:
                    pl.when(stack < stacks - 1)(go)
                else:
                    go()

        prev = None
        for u in units + [None]:
            if u is not None:
                lhs = conv(u)
            znew, g = [], []
            for c in range(gate // CHUNK):
                if u is not None:
                    znew.append(conv_chunk(u, lhs, c))
                if prev is not None:
                    g.append(gated(prev[0], prev[1][c], c))
            if prev is not None:
                finish(prev[0], g)
                k, r0, _ = prev[0]
                if r0 == 0 and (k == cycle // 2 - 1 or k == cycle - 1):
                    @pl.when(stack < stacks - 1)
                    def _():
                        for kk in range(0 if k < cycle // 2 else cycle // 2, k + 1):
                            for cp in weight_copies(stack + 1, kk):
                                cp.start()
            prev = (u, znew)
        for k in range(1, cycle):
            for p in range(len(pieces(k))):
                send(stack, k, p).wait_send()
        return carry

    lo = rows - halo_rows(0)
    stage[0:halo_rows(0), :] = hbuf[lo:rows, :]
    send(0, 0, 0).start()
    lax.fori_loop(0, stacks, body, 0)
    send(stacks - 1, 0, 0).wait_send()

    h_copy = pltpu.make_async_copy(hbuf, hout_ref, out_sem.at[0])
    h_copy.start()
    a = jnp.maximum(skip[...], 0.0).astype(bf16)
    m = jnp.dot(a, w1_ref[...], preferred_element_type=f32) + c1_ref[...]
    m = jnp.maximum(m, 0.0).astype(bf16)
    skip[...] = jnp.dot(m, w2_ref[...], preferred_element_type=f32) + c2_ref[...]
    y_copy = pltpu.make_async_copy(skip, y_ref, out_sem.at[1])
    y_copy.start()
    h_copy.wait()
    y_copy.wait()


def solution(mesh):
    n_sp = mesh.shape["sp"]
    row_spec = P(("ens", "sp"), None)

    def local_stack(x_seq, w_past, w_now, b_conv, w_res, w_skip, w_out1, b_out1, w_out2, b_out2):
        rows, res_ch = x_seq.shape
        stacks, cycle = w_past.shape[:2]
        skip_ch = w_skip.shape[-1]
        gate = w_res.shape[2]
        max_pieces = max(1, 2 ** (cycle - 1) // ROWS)
        vmem = pl.BlockSpec(memory_space=pltpu.VMEM)
        hbm = pl.BlockSpec(memory_space=pl.ANY)
        bf16, f32 = jnp.bfloat16, jnp.float32
        scratch = [
            pltpu.VMEM((rows, res_ch), bf16),
            pltpu.VMEM((rows, skip_ch), f32),
            pltpu.VMEM((cycle, res_ch, 2 * gate), bf16),
            pltpu.VMEM((cycle, res_ch, 2 * gate), bf16),
            pltpu.VMEM((cycle, gate, res_ch), bf16),
            pltpu.VMEM((cycle, gate, skip_ch), bf16),
            pltpu.VMEM((sum(halo_rows(k) for k in range(cycle)), res_ch), bf16),
        ]
        scratch += [pltpu.VMEM((stacks, halo_rows(k), res_ch), bf16) for k in range(cycle)]
        scratch += [
            pltpu.SemaphoreType.DMA,
            pltpu.SemaphoreType.DMA((cycle, 4)),
            pltpu.SemaphoreType.DMA((cycle, max_pieces)),
            pltpu.SemaphoreType.DMA((stacks, cycle, max_pieces)),
            pltpu.SemaphoreType.DMA((2,)),
        ]
        macs = rows * (4 * res_ch * gate + gate * (res_ch + skip_ch))
        return pl.pallas_call(
            functools.partial(wavenet_kernel, n_sp, stacks, cycle),
            out_shape=(jax.ShapeDtypeStruct((rows, w_out2.shape[-1]), f32),
                       jax.ShapeDtypeStruct((rows, res_ch), bf16)),
            in_specs=[hbm, hbm, hbm, vmem, hbm, hbm, vmem, vmem, vmem, vmem],
            out_specs=(hbm, hbm),
            scratch_shapes=scratch,
            compiler_params=pltpu.CompilerParams(collective_id=0, has_side_effects=True,
                                                 vmem_limit_bytes=60 * 1024 * 1024),
            cost_estimate=pl.CostEstimate(flops=2 * macs * stacks * cycle, bytes_accessed=90 * 2 ** 20,
                                          transcendentals=0),
            name="wavenet",
        )(x_seq, w_past, w_now, b_conv, w_res, w_skip, w_out1, b_out1.reshape(1, -1), w_out2, b_out2.reshape(1, -1))

    return jax.shard_map(
        local_stack,
        mesh=mesh,
        in_specs=(row_spec, P(), P(), P(), P(), P(), P(), P(), P(), P()),
        out_specs=(row_spec, row_spec),
        check_vma=False,
    )
```

profile of v0, /device:TPU:98, one launch (start us, length us, event | category | flops | bytes accessed | tf_op | source)
XLA Modules:
  0.0 100.0 jit_solution(452039193306657878)
XLA Ops:
  0.6 1.7 %copy.12.b_ref = f32[3,10,1024]{2,1,0:T(8,128)} copy(f32[3,10,1024]{2,0,1:T(4,128)} %param.13) | data formatting | bytes 245760 | tf_op args[3]
  2.3 93.9 %wavenet.1 = (f32[512,256]{1,0:T(8,128)}, bf16[512,512]{1,0:T(8,128)(2,1)}) custom-call(bf16[512,512]{1,0:T(8,128)(2,1)} %x_ref.1, bf16[3,10,512,1024]{3,2,1,0:T(8,128)(2,1)} %wp_ref.1, bf16[3,10,512,1024]{3,2,1,0:T(8,128)(2,1)} %wn_ref.1, f32[3,10,1024]{2,1,0:T(8,128)} %copy.12.b_ref, bf16[3,10,512,512]{3,2,1,0:T(8,128)(2,1)} %wr_ref.1, ...), custom_call_target="tpu_custom_call" | custom-call | flops 44291850240 | bytes 94371840 | tf_op jit(solution)/shard_map/wavenet/pallas_call | solution.py:245
  96.2 1.9 %copy.15 = f32[512,256]{1,0:T(8,128)} copy(f32[512,256]{1,0:T(8,128)} %get-tuple-element.4) | data formatting | bytes 1048576
  98.1 1.9 %copy.16 = bf16[512,512]{1,0:T(8,128)(2,1)} copy(bf16[512,512]{1,0:T(8,128)(2,1)} %get-tuple-element.5) | data formatting | bytes 1048576
where the time goes:
time: 100 us
  Pallas kernels  93.9 us (94%)
  local copies, waits for them, and re-layouts  5.41 us (5%)
    pallas_call x1, Pallas kernels, local_stack(): pl.pallas_call(functools.partial(wavenet_kernel, n_sp, stacks, cycle), ou...  93.9 us
    unnamed x3, local copies, waits for them, and re-layouts  5.41 us

commit v1 on v0

v1 whole, which is shorter than its diff:
```python
import functools

import jax
import jax.numpy as jnp
from jax import lax
from jax.experimental import pallas as pl
from jax.experimental.pallas import tpu as pltpu
from jax.sharding import PartitionSpec as P

TILE = 16
ROWS = 128
CHUNK = 256
PRE = 32
LOOK = 3
VMEM_MIB = 52
MESH = pl.DeviceIdType.MESH


def halo_rows(k):
    return PRE if k == 0 else 2 ** k if 2 ** k >= PRE else 0


def pieces(rows, k):
    lo, hi, out = rows - halo_rows(k), rows, []
    while hi > lo:
        out.append((max(lo, hi - ROWS), hi))
        hi = max(lo, hi - ROWS)
    return out


def schedule(rows):
    def cut(k, *cuts):
        return [(k, a, b) for a, b in zip(cuts[1:], cuts[:-1])]

    q = rows // 4
    items = []
    for k in range(4):
        items += cut(k, rows, 3 * q, 2 * q, q, -PRE)
    items += cut(4, rows, 3 * q, 2 * q, q, 0)
    items += cut(5, rows, 384, 272, 144, 32)
    items += cut(6, rows, 368, 224, 96)
    items += cut(7, rows, 368)
    items += cut(5, 32, 0)
    items += cut(7, 368, 224)
    items += cut(6, 96, 0)
    items += [("skip", (0, 1, 2, 3), 0, 256), ("skip", (0, 1, 2, 3), 256, 512)]
    items += cut(7, 224, 112, 0)
    items += cut(8, rows, 3 * q, 2 * q)
    items += [("skip", (4, 5, 6, 7), 0, 256), ("skip", (4, 5, 6, 7), 256, 512)]
    items += cut(8, 2 * q, q, 0)
    items += [("skip", (8,), 256, 512)]
    items += cut(9, rows, 3 * q, 2 * q, q, 0)
    items += [("skip", (8,), 0, 256)]
    return items


def wavenet_kernel(n_sp, stacks, cycle, x_ref, wp_ref, wn_ref, b_ref, wr_ref, ws_ref,
                   hbuf, skip, bias_v, gbuf, wp, wn, wr, ws, stage, *scratch):
    halo_layers = [k for k in range(cycle) if halo_rows(k)]
    halos = dict(zip(halo_layers, scratch))
    x_sem, b_sem, w_sem, send_sem, recv_sem = scratch[len(halo_layers):]
    me = lax.axis_index("sp")
    ens = lax.axis_index("ens")
    right = lax.rem(me + 1, n_sp)
    left = lax.rem(me + n_sp - 1, n_sp)
    first = me == 0
    rows = hbuf.shape[0] - PRE
    gate = wr.shape[1]
    f32, bf16 = jnp.float32, jnp.bfloat16
    zero = jnp.zeros((), bf16)

    def weight_copies(stack, k, turn=None):
        par = lax.rem(stack if turn is None else turn, 2)
        return [pltpu.make_async_copy(src.at[stack, k], dst, w_sem.at[k, i])
                for i, (src, dst) in enumerate(((wn_ref, wn.at[k]), (wp_ref, wp.at[k]), (wr_ref, wr.at[k]),
                                                (ws_ref, ws.at[par, k])))]

    stage_off = {}
    off = 0
    for k in halo_layers:
        stage_off[k] = off
        off += halo_rows(k)

    def send(stack, k, p):
        a, b = pieces(rows, k)[p]
        lo = rows - halo_rows(k)
        return pltpu.make_async_remote_copy(
            src_ref=stage.at[pl.ds(stage_off[k] + a - lo, b - a)],
            dst_ref=halos[k].at[stack, pl.ds(a - lo, b - a)],
            send_sem=send_sem.at[k, p],
            recv_sem=recv_sem.at[stack, k, p],
            device_id=(ens, right),
            device_id_type=MESH,
        )

    x_copy = pltpu.make_async_copy(x_ref, hbuf.at[pl.ds(PRE, rows)], x_sem)
    x_copy.start()
    b_copy = pltpu.make_async_copy(b_ref, bias_v, b_sem)
    b_copy.start()
    for c in weight_copies(0, 0):
        c.start()

    barrier = pltpu.get_barrier_semaphore()
    for other in (left, right):
        pl.semaphore_signal(barrier, inc=1, device_id=(ens, other), device_id_type=MESH)
    pl.semaphore_wait(barrier, 2)

    for k in range(1, LOOK):
        for c in weight_copies(0, k):
            c.start()
    skip[...] = jnp.zeros_like(skip)
    x_copy.wait()
    b_copy.wait()

    def load(a, b):
        return hbuf[PRE + a:PRE + b, :]

    def masked(v):
        return jnp.where(first, zero, v)

    def past_rows(stack, k, r0, r1):
        d = 2 ** k
        if d >= rows:
            return masked(halos[k][stack, r0:r1, :])
        a, b = r0 - d, r1 - d
        if d >= TILE:
            if halo_rows(k) == 0:
                return load(a, b)
            parts = []
            if a < 0:
                h = halo_rows(k)
                parts.append(masked(halos[k][stack, h + a:h + min(b, 0), :]))
            if b > 0:
                parts.append(load(max(a, 0), b))
            return parts[0] if len(parts) == 1 else jnp.concatenate(parts, axis=0)
        if r0 == -PRE:
            v = load(r0, r1)
            v = jnp.concatenate([jnp.zeros((TILE, v.shape[1]), bf16), v], axis=0)
        else:
            v = load(r0 - TILE, r1)
        v = v.astype(f32)[TILE - d:TILE - d + r1 - r0]
        return v.astype(bf16)

    def body(stack, carry):
        seen, arrived = set(), set()
        version = {r: 0 for r in range(-PRE, rows, TILE)}
        got = {k: set() for k in range(cycle)}
        sent = set()

        def use_weights(k):
            if k in seen:
                return
            seen.add(k)
            nxt = k + LOOK
            ahead = stack if nxt < cycle else jnp.minimum(stack + 1, stacks - 1)
            for c in weight_copies(ahead, nxt % cycle, stack if nxt < cycle else stack + 1):
                c.start()
            for c in weight_copies(stack, k):
                c.wait()

        def missing(unit):
            k, r0, r1 = unit
            if not halo_rows(k):
                return []
            d = halo_rows(k)
            return [p for p, (a, b) in enumerate(pieces(rows, k))
                    if (k, p) not in arrived and r0 - d < b - rows and min(r1 - d, 0) > a - rows]

        def check(unit):
            k, r0, r1 = unit
            d = 2 ** k
            for r in range(max(r0 - (d if d < rows else 0), -PRE if k < 5 else 0) // TILE * TILE, r1, TILE):
                assert version[r] == k or (r < r0 - TILE and r < 0), (unit, r, version[r])

        def wait_halo(unit):
            k = unit[0]
            for p in missing(unit):
                arrived.add((k, p))
                send(stack, k, p).wait_recv()
                if k == 0:
                    hbuf[0:PRE, :] = masked(halos[0][stack])

        def dots(unit, w, lhs):
            k = unit[0]
            return [[jnp.dot(lhs, w[k, :, b + c * CHUNK:b + (c + 1) * CHUNK], preferred_element_type=f32)
                     for b in (0, gate)] for c in range(gate // CHUNK)]

        def gated(unit, z, c):
            k = unit[0]
            bias = bias_v[k, stack]
            zt = z[0] + bias[None, c * CHUNK:(c + 1) * CHUNK]
            zs = z[1] + bias[None, gate + c * CHUNK:gate + (c + 1) * CHUNK]
            sig = 0.5 * jnp.tanh(0.5 * zs) + 0.5
            return (jnp.tanh(zt) * sig).astype(bf16)

        def finish(unit, g):
            k, r0, r1 = unit
            g = jnp.concatenate(g, axis=1)
            h = load(r0, r1).astype(f32) + jnp.dot(g, wr[k], preferred_element_type=f32)
            h = h.astype(bf16)
            if r0 < 0:
                hbuf[PRE + r0:PRE, :] = masked(h[:-r0])
                hbuf[PRE:PRE + r1, :] = h[-r0:]
                gpos = g[-r0:]
            else:
                hbuf[PRE + r0:PRE + r1, :] = h
                gpos = g
            if k == cycle - 1:
                skip[max(r0, 0):r1, :] += jnp.dot(gpos, ws[lax.rem(stack, 2), k], preferred_element_type=f32)
            else:
                gbuf[k, max(r0, 0):r1, :] = gpos
            for r in range(r0, r1, TILE):
                version[r] = k + 1
                got[k].add(r)
            nk = (k + 1) % cycle
            if not halo_rows(nk):
                return
            lo = rows - halo_rows(nk)
            todo = [(p, a, b) for p, (a, b) in enumerate(pieces(rows, nk))
                    if (nk, p) not in sent and all(r in got[k] for r in range(a, b, TILE))]

            def go():
                s, e = max(r0, lo), r1
                if nk == 0:
                    send(stack, nk, 0).wait_send()
                if s < e:
                    stage[stage_off[nk] + s - lo:stage_off[nk] + e - lo, :] = h[s - r0:e - r0]
                for p, a, b in todo:
                    sent.add((nk, p))
                    send(stack + (1 if nk == 0 else 0), nk, p).start()

            if r1 > lo:
                go()

        def skip_sum(ks, r0, r1):
            acc = jnp.dot(gbuf[ks[0], r0:r1, :], ws[lax.rem(stack, 2), ks[0]], preferred_element_type=f32)
            for k in ks[1:]:
                acc = acc + jnp.dot(gbuf[k, r0:r1, :], ws[lax.rem(stack, 2), k], preferred_element_type=f32)
            skip[r0:r1, :] += acc

        chunks = range(gate // CHUNK)
        prev = None

        def flush():
            nonlocal prev
            if prev is not None:
                unit, z = prev
                prev = None
                finish(unit, [gated(unit, z[c], c) for c in chunks])

        plan = schedule(rows)
        for n, item in enumerate(plan):
            if item[0] == "skip":
                skip_sum(*item[1:])
                continue
            k, r0, r1 = item
            use_weights(k)
            for later in plan[n + 1:n + 2]:
                if later[0] != "skip":
                    use_weights(later[0])
            if prev is not None:
                (pk, p0, p1), d = prev[0], 2 ** k
                if pk == k - 1 and max(r0 - (d if d < rows else 0), -PRE) < p1 and p0 < r1:
                    flush()
            if missing(item):
                if k == 0:
                    flush()
                    wait_halo(item)
                    check(item)
                    zn = dots(item, wn, load(r0, r1))
                else:
                    zn = dots(item, wn, load(r0, r1))
                    flush()
                    wait_halo(item)
                    check(item)
                zp = dots(item, wp, past_rows(stack, k, r0, r1))
                z = [[zp[c][i] + zn[c][i] for i in range(2)] for c in chunks]
                flush()
            else:
                check(item)
                past, now = past_rows(stack, k, r0, r1), load(r0, r1)
                zp, zn = dots(item, wp, past), dots(item, wn, now)
                z = [[zp[c][i] + zn[c][i] for i in range(2)] for c in chunks]
                flush()
            prev = (item, z)
        flush()
        for k in halo_layers[1:]:
            for p in range(len(pieces(rows, k))):
                send(stack, k, p).wait_send()
        return carry

    stage[0:PRE, :] = load(rows - PRE, rows)
    send(0, 0, 0).start()
    lax.fori_loop(0, stacks, body, 0)
    send(stacks, 0, 0).wait()
    for k in range(LOOK):
        for c in weight_copies(stacks - 1, k, stacks):
            c.wait()


def head_kernel(hbuf, skip, w1_ref, c1_ref, w2_ref, c2_ref, y_ref, hout_ref, logits, sems):
    f32, bf16 = jnp.float32, jnp.bfloat16
    rows = skip.shape[0]
    h_copy = pltpu.make_async_copy(hbuf.at[pl.ds(PRE, rows)], hout_ref, sems.at[0])
    h_copy.start()
    a = jnp.maximum(skip[...], 0.0).astype(bf16)
    m = jnp.dot(a, w1_ref[...], preferred_element_type=f32) + c1_ref[...]
    m = jnp.maximum(m, 0.0).astype(bf16)
    logits[...] = jnp.dot(m, w2_ref[...], preferred_element_type=f32) + c2_ref[...]
    y_copy = pltpu.make_async_copy(logits, y_ref, sems.at[1])
    y_copy.start()
    h_copy.wait()
    y_copy.wait()


def solution(mesh):
    n_sp = mesh.shape["sp"]
    row_spec = P(("ens", "sp"), None)

    def local_stack(x_seq, w_past, w_now, b_conv, w_res, w_skip, w_out1, b_out1, w_out2, b_out2):
        rows, res_ch = x_seq.shape
        stacks, cycle = w_past.shape[:2]
        skip_ch = w_skip.shape[-1]
        gate = w_res.shape[2]
        max_pieces = max(1, 2 ** (cycle - 1) // ROWS)
        vmem = pl.BlockSpec(memory_space=pltpu.VMEM)
        hbm = pl.BlockSpec(memory_space=pltpu.HBM)
        bf16, f32 = jnp.bfloat16, jnp.float32
        scratch = [
            pltpu.VMEM((cycle, stacks, 2 * gate), f32),
            pltpu.VMEM((cycle - 1, rows, gate), bf16),
            pltpu.VMEM((cycle, res_ch, 2 * gate), bf16),
            pltpu.VMEM((cycle, res_ch, 2 * gate), bf16),
            pltpu.VMEM((cycle, gate, res_ch), bf16),
            pltpu.VMEM((2, cycle, gate, skip_ch), bf16),
            pltpu.VMEM((sum(halo_rows(k) for k in range(cycle)), res_ch), bf16),
        ]
        scratch += [pltpu.VMEM((stacks + (k == 0), halo_rows(k), res_ch), bf16) for k in range(cycle) if halo_rows(k)]
        scratch += [
            pltpu.SemaphoreType.DMA,
            pltpu.SemaphoreType.DMA,
            pltpu.SemaphoreType.DMA((cycle, 4)),
            pltpu.SemaphoreType.DMA((cycle, max_pieces)),
            pltpu.SemaphoreType.DMA((stacks + 1, cycle, max_pieces)),
        ]
        macs = rows * (4 * res_ch * gate + gate * (res_ch + skip_ch))
        hidden, skip = pl.pallas_call(
            functools.partial(wavenet_kernel, n_sp, stacks, cycle),
            out_shape=(jax.ShapeDtypeStruct((PRE + rows, res_ch), bf16),
                       jax.ShapeDtypeStruct((rows, skip_ch), f32)),
            in_specs=[hbm] * 6,
            out_specs=(vmem, vmem),
            scratch_shapes=scratch,
            compiler_params=pltpu.CompilerParams(collective_id=0, has_side_effects=True,
                                                 vmem_limit_bytes=VMEM_MIB * 2 ** 20),
            cost_estimate=pl.CostEstimate(flops=2 * macs * stacks * cycle, bytes_accessed=90 * 2 ** 20,
                                          transcendentals=0),
            name="wavenet",
        )(x_seq, w_past, w_now, jnp.transpose(b_conv, (1, 0, 2)), w_res, w_skip)
        return pl.pallas_call(
            head_kernel,
            out_shape=(jax.ShapeDtypeStruct((rows, w_out2.shape[-1]), f32),
                       jax.ShapeDtypeStruct((rows, res_ch), bf16)),
            in_specs=[vmem] * 6,
            out_specs=(hbm, hbm),
            scratch_shapes=[pltpu.VMEM((rows, w_out2.shape[-1]), f32), pltpu.SemaphoreType.DMA((2,))],
            compiler_params=pltpu.CompilerParams(vmem_limit_bytes=8 * 2 ** 20),
            name="head",
        )(hidden, skip, w_out1, b_out1.reshape(1, -1), w_out2, b_out2.reshape(1, -1))

    return jax.shard_map(
        local_stack,
        mesh=mesh,
        in_specs=(row_spec, P(), P(), P(), P(), P(), P(), P(), P(), P()),
        out_specs=(row_spec, row_spec),
        check_vma=False,
    )
```

time: 100 us -> 83 us (0.83)
  the two profiles are of different devices: /device:TPU:98 before, /device:TPU:96 now
where the time goes in v1:
time: 83 us; the launch traced here: 82.8 us
  Pallas kernels  80.2 us (97%)
  local copies, waits for them, and re-layouts  1.96 us (2%)
    pallas_call x1, Pallas kernels, local_stack(): pl.pallas_call(functools.partial(wavenet_kernel, n_sp, stacks, cycle), ou...  79 us
    unnamed x12, local copies, waits for them, and re-layouts  1.96 us

profile of v1, /device:TPU:96, one launch (start us, length us, event | category | flops | bytes accessed | tf_op | source)
XLA Modules:
  0.0 82.8 jit_solution(17262604689346048707)
XLA Ops:
  0.6 0.0 copy-start.4
  0.6 1.0 %copy-done.4 = bf16[512,512]{1,0:T(8,128)(2,1)S(1)} copy-done((bf16[512,512]{1,0:T(8,128)(2,1)S(1)}, bf16[512,512]{1,0:T(8,128)(2,1)}, u32[]{:S(2)}) %copy-start.4) | copy-done | bytes 524312
  1.7 0.0 copy-start.5
  1.7 0.9 %copy-done.5 = f32[3,10,1024]{2,0,1:T(4,128)S(1)} copy-done((f32[3,10,1024]{2,0,1:T(4,128)S(1)}, f32[3,10,1024]{2,0,1:T(4,128)}, u32[]{:S(2)}) %copy-start.5) | copy-done | bytes 122904
  2.6 0.0 copy-start
  2.6 0.0 copy-start.1
  2.6 0.0 copy-start.2
  2.6 0.0 copy-start.3
  2.6 79.0 %wavenet.1 = (bf16[544,512]{1,0:T(8,128)(2,1)S(1)}, f32[512,256]{1,0:T(8,128)S(1)}) custom-call(bf16[512,512]{1,0:T(8,128)(2,1)S(1)} %copy-done.4, bf16[3,10,512,1024]{3,2,1,0:T(8,128)(2,1)} %wp_ref.1, bf16[3,10,512,1024]{3,2,1,0:T(8,128)(2,1)} %wn_ref.1, f32[10,3,1024]{2,1,0:T(4,128)S(1)} %bitcast.5, bf16[3,10,512,512]{3,2,1,0:T(8,128)(2,1)} %wr_ref.1, ...), custom_call_target="tpu_custom_call" | custom-call | flops 44291850240 | bytes 94371840 | tf_op jit(solution)/shard_map/wavenet/pallas_call | solution.py:347
  81.6 0.0 copy-done
  81.6 0.0 copy-done.1
  81.6 0.0 copy-done.2
  81.6 0.0 copy-done.3
  81.6 1.2 %head.1 = (f32[512,256]{1,0:T(8,128)}, bf16[512,512]{1,0:T(8,128)(2,1)}) custom-call(bf16[544,512]{1,0:T(8,128)(2,1)S(1)} %get-tuple-element.4.hbuf, f32[512,256]{1,0:T(8,128)S(1)} %get-tuple-element.5.skip, bf16[256,256]{1,0:T(8,128)(2,1)S(1)} %copy-done, f32[1,256]{1,0:T(1,128)S(1)} %bitcast.3, bf16[256,256]{1,0:T(8,128)(2,1)S(1)} %copy-done.1, ...), custom_call_target="tpu_custom_call" | custom-call | tf_op jit(solution)/shard_map/head/pallas_call | solution.py:360
Async XLA Ops:
  0.6 1.0 %copy-start.4 = (bf16[512,512]{1,0:T(8,128)(2,1)S(1)}, bf16[512,512]{1,0:T(8,128)(2,1)}, u32[]{:S(2)}) copy-start(bf16[512,512]{1,0:T(8,128)(2,1)} %x_ref.1) | copy-start | bytes 1572868
  1.7 0.9 %copy-start.5 = (f32[3,10,1024]{2,0,1:T(4,128)S(1)}, f32[3,10,1024]{2,0,1:T(4,128)}, u32[]{:S(2)}) copy-start(f32[3,10,1024]{2,0,1:T(4,128)} %param.13) | copy-start | bytes 368644
  2.6 79.0 %copy-start = (bf16[256,256]{1,0:T(8,128)(2,1)S(1)}, bf16[256,256]{1,0:T(8,128)(2,1)}, u32[]{:S(2)}) copy-start(bf16[256,256]{1,0:T(8,128)(2,1)} %w1_ref.1) | copy-start | bytes 393220
  2.6 79.0 %copy-start.1 = (bf16[256,256]{1,0:T(8,128)(2,1)S(1)}, bf16[256,256]{1,0:T(8,128)(2,1)}, u32[]{:S(2)}) copy-start(bf16[256,256]{1,0:T(8,128)(2,1)} %w2_ref.1) | copy-start | bytes 393220
  2.6 79.0 %copy-start.2 = (f32[256]{0:T(256)S(1)}, f32[256]{0:T(256)}, u32[]{:S(2)}) copy-start(f32[256]{0:T(256)} %param.17) | copy-start | bytes 3076
  2.6 79.0 %copy-start.3 = (f32[256]{0:T(256)S(1)}, f32[256]{0:T(256)}, u32[]{:S(2)}) copy-start(f32[256]{0:T(256)} %param.19) | copy-start | bytes 3076

commit v2 on v1

--- a/solution.py
+++ b/solution.py
@@ -11,8 +11,9 @@
 ROWS = 128
 CHUNK = 256
 PRE = 32
+LATE = (7, 8, 9)
 LOOK = 3
-VMEM_MIB = 52
+VMEM_MIB = 58
 MESH = pl.DeviceIdType.MESH
 
 
@@ -43,14 +44,14 @@
     items += cut(5, 32, 0)
     items += cut(7, 368, 224)
     items += cut(6, 96, 0)
-    items += [("skip", (0, 1, 2, 3), 0, 256), ("skip", (0, 1, 2, 3), 256, 512)]
     items += cut(7, 224, 112, 0)
     items += cut(8, rows, 3 * q, 2 * q)
-    items += [("skip", (4, 5, 6, 7), 0, 256), ("skip", (4, 5, 6, 7), 256, 512)]
+    items += [("skip", (0, 1, 2, 3), 0, 256), ("skip", (0, 1, 2, 3), 256, 512)]
     items += cut(8, 2 * q, q, 0)
-    items += [("skip", (8,), 256, 512)]
-    items += cut(9, rows, 3 * q, 2 * q, q, 0)
+    items += [("skip", (4, 5, 6, 7, 8), 256, 512), ("skip", (4, 5, 6, 7), 0, 256)]
+    items += cut(9, rows, 3 * q)
     items += [("skip", (8,), 0, 256)]
+    items += cut(9, 3 * q, 2 * q, q, 0)
     return items
 
 
@@ -61,8 +62,9 @@
     x_sem, b_sem, w_sem, send_sem, recv_sem = scratch[len(halo_layers):]
     me = lax.axis_index("sp")
     ens = lax.axis_index("ens")
-    right = lax.rem(me + 1, n_sp)
-    left = lax.rem(me + n_sp - 1, n_sp)
+    last = lax.div(me, n_sp - 1)
+    target = me + 1 - 2 * last
+    spare = stacks + 1
     first = me == 0
     rows = hbuf.shape[0] - PRE
     gate = wr.shape[1]
@@ -85,14 +87,22 @@
         a, b = pieces(rows, k)[p]
         lo = rows - halo_rows(k)
         return pltpu.make_async_remote_copy(
-            src_ref=stage.at[pl.ds(stage_off[k] + a - lo, b - a)],
-            dst_ref=halos[k].at[stack, pl.ds(a - lo, b - a)],
-            send_sem=send_sem.at[k, p],
-            recv_sem=recv_sem.at[stack, k, p],
-            device_id=(ens, right),
+            src_ref=stage.at[stack, pl.ds(stage_off[k] + a - lo, b - a)],
+            dst_ref=halos[k].at[stack + spare * last, pl.ds(a - lo, b - a)],
+            send_sem=send_sem.at[stack, k, p],
+            recv_sem=recv_sem.at[stack + spare * last, k, p],
+            device_id=(ens, target),
             device_id_type=MESH,
         )
 
+    def arrival(slot, k, p):
+        a, b = pieces(rows, k)[p]
+        lo = rows - halo_rows(k)
+        return pltpu.make_async_copy(x_ref.at[pl.ds(a - lo, b - a)], halos[k].at[slot, pl.ds(a - lo, b - a)],
+                                     recv_sem.at[slot, k, p])
+
+    every = [(slot, k, p) for slot in range(stacks + 1) for k in halo_layers if slot < stacks or k == 0
+             for p in range(len(pieces(rows, k)))]
     x_copy = pltpu.make_async_copy(x_ref, hbuf.at[pl.ds(PRE, rows)], x_sem)
     x_copy.start()
     b_copy = pltpu.make_async_copy(b_ref, bias_v, b_sem)
@@ -101,13 +111,25 @@
         c.start()
 
     barrier = pltpu.get_barrier_semaphore()
-    for other in (left, right):
-        pl.semaphore_signal(barrier, inc=1, device_id=(ens, other), device_id_type=MESH)
-    pl.semaphore_wait(barrier, 2)
+
+    @pl.when(me > 0)
+    def _():
+        pl.semaphore_signal(barrier, inc=1, device_id=(ens, me - 1), device_id_type=MESH)
+
+    @pl.when(me == n_sp - 2)
+    def _():
+        pl.semaphore_signal(barrier, inc=1, device_id=(ens, me + 1), device_id_type=MESH)
+
+    pl.semaphore_wait(barrier, 1)
 
     for k in range(1, LOOK):
         for c in weight_copies(0, k):
             c.start()
+    @pl.when(me == 0)
+    def _():
+        for t in every:
+            arrival(*t).start()
+
     skip[...] = jnp.zeros_like(skip)
     x_copy.wait()
     b_copy.wait()
@@ -146,6 +168,7 @@
         version = {r: 0 for r in range(-PRE, rows, TILE)}
         got = {k: set() for k in range(cycle)}
         sent = set()
+        ready = []
 
         def use_weights(k):
             if k in seen:
@@ -176,7 +199,7 @@
             k = unit[0]
             for p in missing(unit):
                 arrived.add((k, p))
-                send(stack, k, p).wait_recv()
+                arrival(stack, k, p).wait()
                 if k == 0:
                     hbuf[0:PRE, :] = masked(halos[0][stack])
 
@@ -221,18 +244,17 @@
 
             def go():
                 s, e = max(r0, lo), r1
-                if nk == 0:
-                    send(stack, nk, 0).wait_send()
                 if s < e:
-                    stage[stage_off[nk] + s - lo:stage_off[nk] + e - lo, :] = h[s - r0:e - r0]
+                    stage[stack + (nk == 0), stage_off[nk] + s - lo:stage_off[nk] + e - lo, :] = h[s - r0:e - r0]
                 for p, a, b in todo:
                     sent.add((nk, p))
-                    send(stack + (1 if nk == 0 else 0), nk, p).start()
+                    ready.append((stack + (1 if nk == 0 else 0), nk, p))
 
             if r1 > lo:
                 go()
 
         def skip_sum(ks, r0, r1):
+            assert all(r in got[k] for k in ks for r in range(r0, r1, TILE)), (ks, r0, r1)
             acc = jnp.dot(gbuf[ks[0], r0:r1, :], ws[lax.rem(stack, 2), ks[0]], preferred_element_type=f32)
             for k in ks[1:]:
                 acc = acc + jnp.dot(gbuf[k, r0:r1, :], ws[lax.rem(stack, 2), k], preferred_element_type=f32)
@@ -240,6 +262,11 @@
 
         chunks = range(gate // CHUNK)
         prev = None
+
+        def start_sends():
+            for t in ready:
+                send(*t).start()
+            ready.clear()
 
         def flush():
             nonlocal prev
@@ -252,6 +279,7 @@
         for n, item in enumerate(plan):
             if item[0] == "skip":
                 skip_sum(*item[1:])
+                start_sends()
                 continue
             k, r0, r1 = item
             use_weights(k)
@@ -262,37 +290,35 @@
                 (pk, p0, p1), d = prev[0], 2 ** k
                 if pk == k - 1 and max(r0 - (d if d < rows else 0), -PRE) < p1 and p0 < r1:
                     flush()
-            if missing(item):
-                if k == 0:
-                    flush()
-                    wait_halo(item)
-                    check(item)
-                    zn = dots(item, wn, load(r0, r1))
-                else:
-                    zn = dots(item, wn, load(r0, r1))
-                    flush()
-                    wait_halo(item)
-                    check(item)
-                zp = dots(item, wp, past_rows(stack, k, r0, r1))
-                z = [[zp[c][i] + zn[c][i] for i in range(2)] for c in chunks]
+            late = k in LATE and missing(item)
+            if k == 0:
+                wait_halo(item)
+            zn = dots(item, wn, load(r0, r1))
+            if late:
                 flush()
-            else:
-                check(item)
-                past, now = past_rows(stack, k, r0, r1), load(r0, r1)
-                zp, zn = dots(item, wp, past), dots(item, wn, now)
-                z = [[zp[c][i] + zn[c][i] for i in range(2)] for c in chunks]
-                flush()
+            start_sends()
+            wait_halo(item)
+            check(item)
+            zp = dots(item, wp, past_rows(stack, k, r0, r1))
+            z = [[zp[c][i] + zn[c][i] for i in range(2)] for c in chunks]
+            flush()
             prev = (item, z)
         flush()
-        for k in halo_layers[1:]:
-            for p in range(len(pieces(rows, k))):
-                send(stack, k, p).wait_send()
+        start_sends()
         return carry
 
-    stage[0:PRE, :] = load(rows - PRE, rows)
+    stage[0, 0:PRE, :] = load(rows - PRE, rows)
     send(0, 0, 0).start()
     lax.fori_loop(0, stacks, body, 0)
-    send(stacks, 0, 0).wait()
+    for t in every:
+        send(*t).wait_send()
+    arrival(stacks, 0, 0).wait()
+
+    @pl.when(me == n_sp - 2)
+    def _():
+        for slot, k, p in every:
+            arrival(slot + spare, k, p).wait()
+
     for k in range(LOOK):
         for c in weight_copies(stacks - 1, k, stacks):
             c.wait()
@@ -333,21 +359,20 @@
             pltpu.VMEM((cycle, res_ch, 2 * gate), bf16),
             pltpu.VMEM((cycle, gate, res_ch), bf16),
             pltpu.VMEM((2, cycle, gate, skip_ch), bf16),
-            pltpu.VMEM((sum(halo_rows(k) for k in range(cycle)), res_ch), bf16),
+            pltpu.VMEM((stacks + 1, sum(halo_rows(k) for k in range(cycle)), res_ch), bf16),
         ]
-        scratch += [pltpu.VMEM((stacks + (k == 0), halo_rows(k), res_ch), bf16) for k in range(cycle) if halo_rows(k)]
+        scratch += [pltpu.VMEM((2 * (stacks + 1), halo_rows(k), res_ch), bf16) for k in range(cycle) if halo_rows(k)]
         scratch += [
             pltpu.SemaphoreType.DMA,
             pltpu.SemaphoreType.DMA,
             pltpu.SemaphoreType.DMA((cycle, 4)),
-            pltpu.SemaphoreType.DMA((cycle, max_pieces)),
             pltpu.SemaphoreType.DMA((stacks + 1, cycle, max_pieces)),
+            pltpu.SemaphoreType.DMA((2 * (stacks + 1), cycle, max_pieces)),
         ]
         macs = rows * (4 * res_ch * gate + gate * (res_ch + skip_ch))
         hidden, skip = pl.pallas_call(
             functools.partial(wavenet_kernel, n_sp, stacks, cycle),
-            out_shape=(jax.ShapeDtypeStruct((PRE + rows, res_ch), bf16),
-                       jax.ShapeDtypeStruct((rows, skip_ch), f32)),
+            out_shape=(pltpu.VMEM((PRE + rows, res_ch), bf16), pltpu.VMEM((rows, skip_ch), f32)),
             in_specs=[hbm] * 6,
             out_specs=(vmem, vmem),
             scratch_shapes=scratch,

time: 83 us -> 78.8 us (0.949)
  the two profiles are of different devices: /device:TPU:96 before, /device:TPU:120 now
where the time goes in v2:
time: 78.8 us; the launch traced here: 78.7 us
  Pallas kernels  78 us (99%)
    pallas_call x1, Pallas kernels, local_stack(): pl.pallas_call(functools.partial(wavenet_kernel, n_sp, stacks, cycle), ou...  76.8 us

profile of v2, /device:TPU:120, one launch (start us, length us, event | category | flops | bytes accessed | tf_op | source)
XLA Modules:
  0.0 78.7 jit_solution(8224643917478531848)
XLA Ops:
  0.6 0.0 copy-start
  0.6 0.0 copy-start.1
  0.7 0.0 copy-start.2
  0.7 0.0 copy-start.3
  0.7 76.8 %wavenet.1 = (bf16[544,512]{1,0:T(8,128)(2,1)S(1)}, f32[512,256]{1,0:T(8,128)S(1)}) custom-call(bf16[512,512]{1,0:T(8,128)(2,1)} %x_ref.1, bf16[3,10,512,1024]{3,2,1,0:T(8,128)(2,1)} %wp_ref.1, bf16[3,10,512,1024]{3,2,1,0:T(8,128)(2,1)} %wn_ref.1, f32[10,3,1024]{2,1,0:T(4,128)} %bitcast.5, bf16[3,10,512,512]{3,2,1,0:T(8,128)(2,1)} %wr_ref.1, ...), custom_call_target="tpu_custom_call" | custom-call | flops 44291850240 | bytes 94371840 | tf_op jit(solution)/shard_map/wavenet/pallas_call | solution.py:373
  77.4 0.0 copy-done
  77.4 0.0 copy-done.1
  77.5 0.0 copy-done.2
  77.5 0.0 copy-done.3
  77.5 1.2 %head.1 = (f32[512,256]{1,0:T(8,128)}, bf16[512,512]{1,0:T(8,128)(2,1)}) custom-call(bf16[544,512]{1,0:T(8,128)(2,1)S(1)} %get-tuple-element.4.hbuf, f32[512,256]{1,0:T(8,128)S(1)} %get-tuple-element.5.skip, bf16[256,256]{1,0:T(8,128)(2,1)S(1)} %copy-done, f32[1,256]{1,0:T(1,128)S(1)} %bitcast.3, bf16[256,256]{1,0:T(8,128)(2,1)S(1)} %copy-done.1, ...), custom_call_target="tpu_custom_call" | custom-call | tf_op jit(solution)/shard_map/head/pallas_call | solution.py:385
Async XLA Ops:
  0.6 76.8 %copy-start = (bf16[256,256]{1,0:T(8,128)(2,1)S(1)}, bf16[256,256]{1,0:T(8,128)(2,1)}, u32[]{:S(2)}) copy-start(bf16[256,256]{1,0:T(8,128)(2,1)} %w1_ref.1) | copy-start | bytes 393220
  0.6 76.8 %copy-start.1 = (bf16[256,256]{1,0:T(8,128)(2,1)S(1)}, bf16[256,256]{1,0:T(8,128)(2,1)}, u32[]{:S(2)}) copy-start(bf16[256,256]{1,0:T(8,128)(2,1)} %w2_ref.1) | copy-start | bytes 393220
  0.7 76.8 %copy-start.2 = (f32[256]{0:T(256)S(1)}, f32[256]{0:T(256)}, u32[]{:S(2)}) copy-start(f32[256]{0:T(256)} %param.17) | copy-start | bytes 3076
  0.7 76.8 %copy-start.3 = (f32[256]{0:T(256)S(1)}, f32[256]{0:T(256)}, u32[]{:S(2)}) copy-start(f32[256]{0:T(256)} %param.19) | copy-start | bytes 3076

commit v3 on v2

--- a/solution.py
+++ b/solution.py
@@ -11,7 +11,7 @@
 ROWS = 128
 CHUNK = 256
 PRE = 32
-LATE = (7, 8, 9)
+LATE = (8, 9)
 LOOK = 3
 VMEM_MIB = 58
 MESH = pl.DeviceIdType.MESH
@@ -46,11 +46,11 @@
     items += cut(6, 96, 0)
     items += cut(7, 224, 112, 0)
     items += cut(8, rows, 3 * q, 2 * q)
-    items += [("skip", (0, 1, 2, 3), 0, 256), ("skip", (0, 1, 2, 3), 256, 512)]
+    items += [("skip", (0, 1, 2, 3), 256, 512)]
     items += cut(8, 2 * q, q, 0)
     items += [("skip", (4, 5, 6, 7, 8), 256, 512), ("skip", (4, 5, 6, 7), 0, 256)]
     items += cut(9, rows, 3 * q)
-    items += [("skip", (8,), 0, 256)]
+    items += [("skip", (0, 1, 2, 3, 8), 0, 256)]
     items += cut(9, 3 * q, 2 * q, q, 0)
     return items
 

time: 78.8 us -> 78.6 us (level)
  no operation moved by 1% of the time
where the time goes in v3:
time: 78.6 us; the launch traced here: 78.5 us
  Pallas kernels  77.8 us (99%)
    pallas_call x1, Pallas kernels, local_stack(): pl.pallas_call(functools.partial(wavenet_kernel, n_sp, stacks, cycle), ou...  76.6 us

profile of v3, /device:TPU:120, one launch (start us, length us, event | category | flops | bytes accessed | tf_op | source)
XLA Modules:
  0.0 78.5 jit_solution(3314165686715705886)
XLA Ops:
  0.6 0.0 copy-start
  0.6 0.0 copy-start.1
  0.7 0.0 copy-start.2
  0.7 0.0 copy-start.3
  0.7 76.6 %wavenet.1 = (bf16[544,512]{1,0:T(8,128)(2,1)S(1)}, f32[512,256]{1,0:T(8,128)S(1)}) custom-call(bf16[512,512]{1,0:T(8,128)(2,1)} %x_ref.1, bf16[3,10,512,1024]{3,2,1,0:T(8,128)(2,1)} %wp_ref.1, bf16[3,10,512,1024]{3,2,1,0:T(8,128)(2,1)} %wn_ref.1, f32[10,3,1024]{2,1,0:T(4,128)} %bitcast.5, bf16[3,10,512,512]{3,2,1,0:T(8,128)(2,1)} %wr_ref.1, ...), custom_call_target="tpu_custom_call" | custom-call | flops 44291850240 | bytes 94371840 | tf_op jit(solution)/shard_map/wavenet/pallas_call | solution.py:373
  77.3 0.0 copy-done
  77.3 0.0 copy-done.1
  77.3 0.0 copy-done.2
  77.3 0.0 copy-done.3
  77.3 1.2 %head.1 = (f32[512,256]{1,0:T(8,128)}, bf16[512,512]{1,0:T(8,128)(2,1)}) custom-call(bf16[544,512]{1,0:T(8,128)(2,1)S(1)} %get-tuple-element.4.hbuf, f32[512,256]{1,0:T(8,128)S(1)} %get-tuple-element.5.skip, bf16[256,256]{1,0:T(8,128)(2,1)S(1)} %copy-done, f32[1,256]{1,0:T(1,128)S(1)} %bitcast.3, bf16[256,256]{1,0:T(8,128)(2,1)S(1)} %copy-done.1, ...), custom_call_target="tpu_custom_call" | custom-call | tf_op jit(solution)/shard_map/head/pallas_call | solution.py:385
Async XLA Ops:
  0.6 76.7 %copy-start = (bf16[256,256]{1,0:T(8,128)(2,1)S(1)}, bf16[256,256]{1,0:T(8,128)(2,1)}, u32[]{:S(2)}) copy-start(bf16[256,256]{1,0:T(8,128)(2,1)} %w1_ref.1) | copy-start | bytes 393220
  0.6 76.7 %copy-start.1 = (bf16[256,256]{1,0:T(8,128)(2,1)S(1)}, bf16[256,256]{1,0:T(8,128)(2,1)}, u32[]{:S(2)}) copy-start(bf16[256,256]{1,0:T(8,128)(2,1)} %w2_ref.1) | copy-start | bytes 393220
  0.7 76.7 %copy-start.2 = (f32[256]{0:T(256)S(1)}, f32[256]{0:T(256)}, u32[]{:S(2)}) copy-start(f32[256]{0:T(256)} %param.17) | copy-start | bytes 3076
  0.7 76.7 %copy-start.3 = (f32[256]{0:T(256)S(1)}, f32[256]{0:T(256)}, u32[]{:S(2)}) copy-start(f32[256]{0:T(256)} %param.19) | copy-start | bytes 3076
